TPU v7x, 32 devices: a whole 2x2x4 slice. The times are simulated.
32 devices in a mesh: blk: 16 (over z, y, x), ga: 2 (over core).
Axes of the slice: x: 2, y: 2, z: 4, core: 2. Of those that a mesh axis runs over, the one named last changes fastest.
Arguments:
- pair_elements: bfloat16 [4096, 16384], P('ga', 'blk'), may hold values from -6 to 6
- screening: bfloat16 [4096, 4096], P('ga', 'blk'), may hold values from -0.09375 to 0.09375
- energies: float32 [256], replicated, may hold values from 0.5 to 3
- frequencies: float32 [8], replicated, may hold values from 0.3 to 3
- qp_index: int32 [32], replicated, may hold values from 0 to 255
- occupied: int32 [256], replicated, may hold values 0 or 1
Outputs:
- self_energy: float32 [2, 8, 32, 32], replicated
All inputs are finite; a program needn't handle non-finite values.
Results may differ from a plain program's by a relative error of at most 0.0003.
Values may be sent and summed in bfloat16 or wider, within the bound.
A program may use at most 128 MiB of HBM per device.

v0:
```python
import jax
import jax.numpy as jnp
from jax import lax
from jax.sharding import PartitionSpec as P

STATES = 32
NG = 4096


def band_weights(energies, frequencies, qp_index, occupied, offset, band_count):
    level_count = energies.shape[0]
    position = jnp.arange(level_count, dtype=jnp.int32)
    signed = jnp.where(occupied == 1, -energies, energies)
    onehot = (qp_index[:, None] == position[None, :]).astype(jnp.float32)
    state_level = jnp.sum(onehot * signed[None, :], axis=1)
    band_level = lax.dynamic_slice_in_dim(signed, offset, band_count, 0)
    detuning = state_level[:, None] - band_level[None, :]
    imag_freq = frequencies[:, None, None]
    modulus = detuning[None] ** 2 + imag_freq**2
    return (detuning[None] / modulus, -imag_freq / modulus)


def window_sigma(elements, screened, weight_real, weight_imag, band_count):
    row_count = elements.shape[0]
    local_elems = elements.astype(jnp.float32).reshape(row_count, band_count, 2, STATES)
    image_cols = screened.reshape(row_count, band_count, 2, STATES)
    intersection = jnp.einsum(
        "gnpi,gnqj->npiqj", local_elems, image_cols, precision=lax.Precision.HIGHEST
    )
    intersection_real = intersection[:, 0, :, 0, :] + intersection[:, 1, :, 1, :]
    intersection_imag = intersection[:, 0, :, 1, :] - intersection[:, 1, :, 0, :]
    sigma_real = jnp.einsum(
        "kin,nij->kij", weight_real, intersection_real, precision=lax.Precision.HIGHEST
    ) - jnp.einsum("kin,nij->kij", weight_imag, intersection_imag, precision=lax.Precision.HIGHEST)
    sigma_imag = jnp.einsum(
        "kin,nij->kij", weight_real, intersection_imag, precision=lax.Precision.HIGHEST
    ) + jnp.einsum("kin,nij->kij", weight_imag, intersection_real, precision=lax.Precision.HIGHEST)
    return jnp.stack([sigma_real, sigma_imag]) / NG


def shards(pair_elements, screening, energies, frequencies, qp_index, occupied):
    col_count = pair_elements.shape[1]
    band_count = col_count // (2 * STATES)
    gathered = lax.all_gather(pair_elements, "ga", axis=0, tiled=True)
    screened = jnp.dot(
        lax.all_gather(screening, "blk", axis=1, tiled=True),
        gathered,
        preferred_element_type=jnp.float32,
    )
    band_start = lax.axis_index("blk") * band_count
    weight_real, weight_imag = band_weights(
        energies, frequencies, qp_index, occupied, band_start, band_count
    )
    partial_value = window_sigma(pair_elements, screened, weight_real, weight_imag, band_count)
    return lax.psum(partial_value, ("blk", "ga"))


def solution(mesh):
    placed = (P("ga", "blk"), P("ga", "blk"), P(), P(), P(), P())
    return jax.shard_map(shards, mesh=mesh, in_specs=placed, out_specs=P(), check_vma=False)
```

profile of v0, /device:TPU:0, one launch (start us, length us, event | category | flops | bytes accessed | tf_op | source)
XLA Modules:
  0.0 443.0 jit_solution(11646669424119894896)
XLA Ops:
  6.5 0.0 copy-start.1
  6.5 0.0 copy-start.2
  6.5 0.0 copy-start.3
  6.5 0.0 copy-start.4
  6.5 0.0 all-gather.5.cloned.1.call-start
  6.6 0.7 all-gather.5.cloned.1.call-update
  7.3 0.0 all-gather.3.cloned.1.call-start
  7.3 0.7 all-gather.3.cloned.1.call-update
  8.0 0.0 all-reduce.2.cloned.1.call-start
  8.1 6.6 %copy.19 = bf16[2048,1024]{0,1:T(8,128)(2,1)} copy(bf16[2048,1024]{1,0:T(8,128)(2,1)} %param.6) | data formatting | bytes 8388608 | tf_op args[0]
  14.7 0.0 copy-done.1
  14.7 0.0 copy-done.2
  14.7 0.1 dynamic_slice.3
  14.7 0.0 copy-done.3
  14.8 0.2 select_reduce_fusion
  14.9 0.0 copy-done.4
  14.9 0.1 broadcast_subtract_fusion
  15.0 16.5 %all-gather.5.cloned.1.call-done = bf16[4096,1024]{1,0:T(8,128)(2,1)} async-done(((bf16[2048,1024]{1,0:T(8,128)(2,1)}), bf16[4096,1024]{1,0:T(8,128)(2,1)}) %all-gather.5.cloned.1.call-update) | async-done | bytes 8388624 | tf_op jit(solution)/shard_map/all_gather | solution.py:44
  31.5 238.5 %all-gather.3.cloned.1.call-done = bf16[2048,4096]{1,0:T(8,128)(2,1)} async-done(((bf16[2048,256]{1,0:T(8,128)(2,1)}), bf16[2048,4096]{1,0:T(8,128)(2,1)}) %all-gather.3.cloned.1.call-update) | async-done | bytes 16777232 | tf_op jit(solution)/shard_map/all_gather | solution.py:46
  270.0 0.0 copy-start
  270.0 24.3 %fusion.20 = f32[2048,1024]{0,1:T(8,128)} fusion(bf16[2048,4096]{1,0:T(8,128)(2,1)} %all-gather.3.cloned.1.call-done, bf16[4096,1024]{1,0:T(8,128)(2,1)} %all-gather.5.cloned.1.call-done), kind=kOutput, calls=%fused_computation.32 | convolution fusion | flops 17179869184 | bytes 33554432 | tf_op jit(solution)/shard_map/dot_general | solution.py:45
  294.3 0.0 copy-done
  294.3 12.7 %convolution_bitcast_fusion = f32[16,2,32,2,32]{2,4,1,3,0:T(8,128)S(1)} fusion(f32[2048,16,2,32,1]{0,3,4,2,1:T(8,128)} %bitcast.33, bf16[2048,16,2,32,1]{0,3,2,4,1:T(8,128)(2,1)S(1)} %bitcast.32), kind=kOutput, calls=%fused_computation | convolution fusion | flops 1610612736 | bytes 12845056 | tf_op jit(solution)/shard_map/gnpi,gnqj->npiqj/dot_general | solution.py:27
  307.0 0.1 fusion.3
  307.1 0.2 copy.21
  307.3 0.2 copy.20
  307.4 0.4 fusion.4
  307.9 0.4 fusion.5
  308.3 0.4 fusion
  308.7 0.4 fusion.1
  309.1 0.7 maximum_multiply_fusion
  309.9 0.0 all-reduce.2.cloned.1.call-update
  309.9 124.9 %all-reduce.2.cloned.1.call-done = f32[2,8,32,32]{3,1,2,0:T(8,128)} async-done(((f32[2,8,32,32]{3,1,2,0:T(8,128)}), f32[2,8,32,32]{3,1,2,0:T(8,128)}) %all-reduce.2.cloned.1.call-update) | async-done | bytes 65552 | tf_op jit(solution)/shard_map/psum | solution.py:55
  434.8 1.7 copy.24
  (2 shorter events, 0.0 us)
Async XLA Ops:
  6.5 8.1 %copy-start.1 = (f32[256]{0:T(256)S(1)}, f32[256]{0:T(256)}, u32[]{:S(2)}) copy-start(f32[256]{0:T(256)} %param.8) | copy-start | bytes 3076
  6.5 8.1 %copy-start.2 = (s32[256]{0:T(256)S(1)}, s32[256]{0:T(256)}, u32[]{:S(2)}) copy-start(s32[256]{0:T(256)} %param.11) | copy-start | bytes 3076
  6.5 8.2 %copy-start.3 = (s32[32]{0:T(128)S(1)}, s32[32]{0:T(128)}, u32[]{:S(2)}) copy-start(s32[32]{0:T(128)} %param.10) | copy-start | bytes 388
  6.5 8.4 %copy-start.4 = (f32[8]{0:T(128)S(1)}, f32[8]{0:T(128)}, u32[]{:S(2)}) copy-start(f32[8]{0:T(128)} %param.9) | copy-start | bytes 100
  6.5 25.0 %all-gather.5.cloned.1.call-start = ((), (), s32[]{:S(2)}) async-start(), calls=%async_computation.1 | async-start | bytes 12582912 | tf_op jit(solution)/shard_map/all_gather | solution.py:44
  7.3 262.8 %all-gather.3.cloned.1.call-start = ((), (), s32[]{:S(2)}) async-start(), calls=%async_computation | async-start | bytes 17825792 | tf_op jit(solution)/shard_map/all_gather | solution.py:46
  8.0 426.8 %all-reduce.2.cloned.1.call-start = ((), (), s32[]{:S(2)}) async-start(), calls=%async_computation.2 | async-start | bytes 524288 | tf_op jit(solution)/shard_map/psum | solution.py:55
  270.0 24.3 %copy-start = (bf16[2048,1024]{0,1:T(8,128)(2,1)S(1)}, bf16[2048,1024]{0,1:T(8,128)(2,1)}, u32[]{:S(2)}) copy-start(bf16[2048,1024]{0,1:T(8,128)(2,1)} %copy.19) | copy-start | bytes 12582916
Sparse Core Ops, SparseCore 0:
  8.9 22.5 all-gather.4
  34.2 235.7 all-gather.2
  310.0 124.7 all-reduce.1
where the time goes:
time: 443 us
  waiting for transfers between devices  381 us (86%)
  matrix products  38.6 us (9%)
  between operations  13.2 us (3%)
  local copies, waits for them, and re-layouts  8.72 us (2%)
    all_gather x1, waiting for transfers between devices, shards(): lax.all_gather(screening, 'blk', axis=1, tiled=True)  239 us
    psum x1, waiting for transfers between devices, shards(): return lax.psum(partial_value, ('blk', 'ga'))  125 us
    dot_general x1, matrix products, shards(): jnp.dot(lax.all_gather(screening, 'blk', axis=1, tiled=True), gathered, p...  24.3 us
    all_gather x1, waiting for transfers between devices, shards(): gathered = lax.all_gather(pair_elements, 'ga', axis=0, tiled=True)  16.5 us
    dot_general x1, matrix products, window_sigma(): jnp.einsum('gnpi,gnqj->npiqj', local_elems, image_cols, precision=lax.Pre...  12.7 us
  transfers between devices with their start and end apart: 3, of which 3 were waited for; matrix products, arithmetic and copies ran while one was open for 2% of the time, Pallas kernels for 0%

commit v1 on v0

--- a/solution.py
+++ b/solution.py
@@ -52,7 +52,7 @@
         energies, frequencies, qp_index, occupied, band_start, band_count
     )
     partial_value = window_sigma(pair_elements, screened, weight_real, weight_imag, band_count)
-    return lax.psum(partial_value, ("blk", "ga"))
+    return jnp.sum(lax.all_gather(partial_value, ("blk", "ga")), axis=0)
 
 
 def solution(mesh):

time: 443 us -> 397 us (0.90)
  waiting for transfers between devices: 381 us -> 332 us
  other arithmetic: 1.07 us -> 5.53 us
    psum x1 -> x0, waiting for transfers between devices: 125 us -> none  [shards(): return lax.psum(partial_value, ('blk', 'ga'))]
    all_gather x0 -> x1, waiting for transfers between devices: none -> 75.4 us  [shards(): return jnp.sum(lax.all_gather(partial_value, ('blk', 'ga')), axis=0)]
    reduce_sum x0 -> x1, other arithmetic: none -> 5.16 us  [shards(): return jnp.sum(lax.all_gather(partial_value, ('blk', 'ga')), axis=0)]
where the time goes in v1:
time: 397 us
  waiting for transfers between devices  332 us (84%)
  matrix products  38.6 us (10%)
  between operations  13.2 us (3%)
  local copies, waits for them, and re-layouts  7.77 us (2%)
  other arithmetic  5.53 us (1%)
    all_gather x1, waiting for transfers between devices, shards(): lax.all_gather(screening, 'blk', axis=1, tiled=True)  239 us
    all_gather x1, waiting for transfers between devices, shards(): return jnp.sum(lax.all_gather(partial_value, ('blk', 'ga')), axis=0)  75.4 us
    dot_general x1, matrix products, shards(): jnp.dot(lax.all_gather(screening, 'blk', axis=1, tiled=True), gathered, p...  24.3 us
    all_gather x1, waiting for transfers between devices, shards(): gathered = lax.all_gather(pair_elements, 'ga', axis=0, tiled=True)  16.5 us
    dot_general x1, matrix products, window_sigma(): jnp.einsum('gnpi,gnqj->npiqj', local_elems, image_cols, precision=lax.Pre...  12.7 us
  transfers between devices with their start and end apart: 3, of which 3 were waited for; matrix products, arithmetic and copies ran while one was open for 2% of the time, Pallas kernels for 0%

profile of v1, /device:TPU:0, one launch (start us, length us, event | category | flops | bytes accessed | tf_op | source)
XLA Modules:
  0.0 397.0 jit_solution(14370914172628497186)
XLA Ops:
  6.5 0.0 copy-start.1
  6.5 0.0 copy-start.2
  6.5 0.0 copy-start.3
  6.5 0.0 copy-start.4
  6.5 0.0 all-gather.6.cloned.1.call-start
  6.6 0.7 all-gather.6.cloned.1.call-update
  7.3 0.0 all-gather.4.cloned.1.call-start
  7.3 0.7 all-gather.4.cloned.1.call-update
  8.0 0.0 all-gather.8.cloned.1.call-start
  8.1 6.6 %copy.25 = bf16[2048,1024]{0,1:T(8,128)(2,1)} copy(bf16[2048,1024]{1,0:T(8,128)(2,1)} %param.6) | data formatting | bytes 8388608 | tf_op args[0]
  14.7 0.0 copy-done.1
  14.7 0.0 copy-done.2
  14.7 0.1 dynamic_slice.3
  14.7 0.0 copy-done.3
  14.8 0.2 select_reduce_fusion
  14.9 0.0 copy-done.4
  14.9 0.1 broadcast_subtract_fusion
  15.0 16.5 %all-gather.6.cloned.1.call-done = bf16[4096,1024]{1,0:T(8,128)(2,1)} async-done(((bf16[2048,1024]{1,0:T(8,128)(2,1)}), bf16[4096,1024]{1,0:T(8,128)(2,1)}) %all-gather.6.cloned.1.call-update) | async-done | bytes 8388624 | tf_op jit(solution)/shard_map/all_gather | solution.py:44
  31.5 238.5 %all-gather.4.cloned.1.call-done = bf16[2048,4096]{1,0:T(8,128)(2,1)} async-done(((bf16[2048,256]{1,0:T(8,128)(2,1)}), bf16[2048,4096]{1,0:T(8,128)(2,1)}) %all-gather.4.cloned.1.call-update) | async-done | bytes 16777232 | tf_op jit(solution)/shard_map/all_gather | solution.py:46
  270.0 0.0 copy-start
  270.0 24.3 %fusion.20 = f32[2048,1024]{0,1:T(8,128)} fusion(bf16[2048,4096]{1,0:T(8,128)(2,1)} %all-gather.4.cloned.1.call-done, bf16[4096,1024]{1,0:T(8,128)(2,1)} %all-gather.6.cloned.1.call-done), kind=kOutput, calls=%fused_computation.32 | convolution fusion | flops 17179869184 | bytes 33554432 | tf_op jit(solution)/shard_map/dot_general | solution.py:45
  294.3 0.0 copy-done
  294.3 12.7 %convolution_bitcast_fusion = f32[16,2,32,2,32]{2,4,1,3,0:T(8,128)S(1)} fusion(f32[2048,16,2,32,1]{0,3,4,2,1:T(8,128)} %bitcast.33, bf16[2048,16,2,32,1]{0,3,2,4,1:T(8,128)(2,1)S(1)} %bitcast.32), kind=kOutput, calls=%fused_computation | convolution fusion | flops 1610612736 | bytes 12845056 | tf_op jit(solution)/shard_map/gnpi,gnqj->npiqj/dot_general | solution.py:27
  307.0 0.1 fusion.3
  307.1 0.2 copy.27
  307.3 0.2 copy.26
  307.4 0.4 fusion.4
  307.9 0.4 fusion.5
  308.3 0.4 fusion
  308.7 0.4 fusion.1
  309.2 0.8 copy.30
  309.9 0.0 all-gather.8.cloned.1.call-update
  309.9 75.4 %all-gather.8.cloned.1.call-done = f32[32,2,8,32,32]{4,3,2,1,0:T(8,128)} async-done(((f32[1,2,8,32,32]{4,3,2,1,0:T(8,128)}), f32[32,2,8,32,32]{4,3,2,1,0:T(8,128)}) %all-gather.8.cloned.1.call-update) | async-done | bytes 2097168 | tf_op jit(solution)/shard_map/all_gather | solution.py:55
  385.3 5.2 %reduce_sum.19 = f32[2,8,32,32]{3,2,1,0:T(8,128)} reduce(f32[32,2,8,32,32]{4,3,2,1,0:T(8,128)} %all-gather.8.cloned.1.call-done, f32[]{:T(128)} %constant.5.clone.1), dimensions={0}, to_apply=%region_1.2 | reduce | flops 507904 | bytes 2162692 | tf_op jit(solution)/shard_map/reduce_sum | solution.py:55
  (3 shorter events, 0.0 us)
Async XLA Ops:
  6.5 8.1 %copy-start.1 = (f32[256]{0:T(256)S(1)}, f32[256]{0:T(256)}, u32[]{:S(2)}) copy-start(f32[256]{0:T(256)} %param.8) | copy-start | bytes 3076
  6.5 8.1 %copy-start.2 = (s32[256]{0:T(256)S(1)}, s32[256]{0:T(256)}, u32[]{:S(2)}) copy-start(s32[256]{0:T(256)} %param.11) | copy-start | bytes 3076
  6.5 8.2 %copy-start.3 = (s32[32]{0:T(128)S(1)}, s32[32]{0:T(128)}, u32[]{:S(2)}) copy-start(s32[32]{0:T(128)} %param.10) | copy-start | bytes 388
  6.5 8.4 %copy-start.4 = (f32[8]{0:T(128)S(1)}, f32[8]{0:T(128)}, u32[]{:S(2)}) copy-start(f32[8]{0:T(128)} %param.9) | copy-start | bytes 100
  6.5 25.0 %all-gather.6.cloned.1.call-start = ((), (), s32[]{:S(2)}) async-start(), calls=%async_computation.1 | async-start | bytes 12582912 | tf_op jit(solution)/shard_map/all_gather | solution.py:44
  7.3 262.8 %all-gather.4.cloned.1.call-start = ((), (), s32[]{:S(2)}) async-start(), calls=%async_computation | async-start | bytes 17825792 | tf_op jit(solution)/shard_map/all_gather | solution.py:46
  8.0 377.3 %all-gather.8.cloned.1.call-start = ((), (), s32[]{:S(2)}) async-start(), calls=%async_computation.2 | async-start | bytes 8650752 | tf_op jit(solution)/shard_map/all_gather | solution.py:55
  270.0 24.3 %copy-start = (bf16[2048,1024]{0,1:T(8,128)(2,1)S(1)}, bf16[2048,1024]{0,1:T(8,128)(2,1)}, u32[]{:S(2)}) copy-start(bf16[2048,1024]{0,1:T(8,128)(2,1)} %copy.25) | copy-start | bytes 12582916
Sparse Core Ops, SparseCore 0:
  8.9 22.5 all-gather.5
  34.2 235.7 all-gather.3
  310.1 75.2 all-gather.7

commit v2 on v0

--- a/solution.py
+++ b/solution.py
@@ -43,7 +43,7 @@
     band_count = col_count // (2 * STATES)
     gathered = lax.all_gather(pair_elements, "ga", axis=0, tiled=True)
     screened = jnp.dot(
-        lax.all_gather(screening, "blk", axis=1, tiled=True),
+        jnp.concatenate(lax.all_gather(screening, "blk"), axis=1),
         gathered,
         preferred_element_type=jnp.float32,
     )

time: 443 us -> 397 us (0.90)
  waiting for transfers between devices: 381 us -> 315 us
  local copies, waits for them, and re-layouts: 8.72 us -> 31.1 us
    all_gather x1, waiting for transfers between devices: 239 us -> 190 us  [shards(): lax.all_gather(screening, 'blk')]
    reshape x0 -> x1, local copies, waits for them, and re-layouts: none -> 22.4 us  [shards(): jnp.concatenate(lax.all_gather(screening, 'blk'), axis=1)]
    all_gather x1, waiting for transfers between devices: 16.5 us -> 0.01 us  [shards(): gathered = lax.all_gather(pair_elements, 'ga', axis=0, tiled=True)]
  transfers between devices with their start and end apart: 3 -> 3, of which waited for: 3 -> 2; matrix products, arithmetic and copies ran while one was open for 2% -> 7% of each run, Pallas kernels for 0% -> 0%
where the time goes in v2:
time: 397 us; the launch traced here: 396 us
  waiting for transfers between devices  315 us (79%)
  matrix products  35.5 us (9%)
  local copies, waits for them, and re-layouts  31.1 us (8%)
  between operations  13.2 us (3%)
    all_gather x1, waiting for transfers between devices, shards(): lax.all_gather(screening, 'blk')  190 us
    psum x1, waiting for transfers between devices, shards(): return lax.psum(partial_value, ('blk', 'ga'))  125 us
    dot_general x1, matrix products, shards(): jnp.dot(jnp.concatenate(lax.all_gather(screening, 'blk'), axis=1), gather...  23.5 us
    reshape x1, local copies, waits for them, and re-layouts, shards(): jnp.concatenate(lax.all_gather(screening, 'blk'), axis=1)  22.4 us
    dot_general x1, matrix products, window_sigma(): jnp.einsum('gnpi,gnqj->npiqj', local_elems, image_cols, precision=lax.Pre...  10.3 us
  transfers between devices with their start and end apart: 3, of which 2 were waited for; matrix products, arithmetic and copies ran while one was open for 7% of the time, Pallas kernels for 0%

profile of v2, /device:TPU:0, one launch (start us, length us, event | category | flops | bytes accessed | tf_op | source)
XLA Modules:
  0.0 396.4 jit_solution(5900911724425095981)
XLA Ops:
  6.5 0.0 copy-start.1
  6.5 0.0 copy-start.2
  6.5 0.0 copy-start.3
  6.5 0.0 copy-start.4
  6.5 0.0 all-gather.6.cloned.1.call-start
  6.6 0.7 all-gather.6.cloned.1.call-update
  7.3 0.0 all-gather.4.cloned.1.call-start
  7.3 6.5 %copy.30 = bf16[2048,1024]{0,1:T(8,128)(2,1)} copy(bf16[2048,1024]{1,0:T(8,128)(2,1)} %param.6) | data formatting | bytes 8388608 | tf_op args[0]
  13.8 0.0 all-gather.4.cloned.1.call-update
  13.8 0.0 all-reduce.2.cloned.1.call-start
  13.9 0.0 copy-done.1
  13.9 0.0 copy-done.2
  13.9 0.1 dynamic_slice.3
  14.0 0.0 copy-done.3
  14.0 0.2 select_reduce_fusion
  14.2 0.0 copy-done.4
  14.2 0.1 broadcast_subtract_fusion
  14.3 189.6 %all-gather.6.cloned.1.call-done = bf16[32768,256]{1,0:T(8,128)(2,1)} async-done(((bf16[2048,256]{1,0:T(8,128)(2,1)}), bf16[32768,256]{1,0:T(8,128)(2,1)}) %all-gather.6.cloned.1.call-update) | async-done | bytes 16777232 | tf_op jit(solution)/shard_map/all_gather | solution.py:46
  203.9 22.4 %copy.29 = bf16[2048,16,256]{0,2,1:T(8,128)(2,1)} copy(bf16[2048,16,256]{2,0,1:T(8,128)(2,1)} %bitcast.43) | data formatting | bytes 33554432 | tf_op jit(solution)/shard_map/reshape | solution.py:46
  226.3 0.0 all-gather.4.cloned.1.call-done
  226.3 0.0 copy-start
  226.3 23.5 %fusion.25 = f32[2048,16,2,32]{0,3,2,1:T(8,128)S(1)} fusion(bf16[2048,4096,1,1]{0,1,3,2:T(8,128)(2,1)} %bitcast.44, bf16[16,2,32,4096]{3,2,1,0:T(8,128)(2,1)} %bitcast.45), kind=kOutput, calls=%fused_computation.34 | convolution fusion | flops 17179869184 | bytes 33554432 | tf_op jit(solution)/shard_map/dot_general | solution.py:45
  249.8 0.0 copy-done
  249.8 10.3 %fusion.2 = f32[16,2,32,2,32]{2,4,1,3,0:T(8,128)S(1)} fusion(bf16[2048,16,2,32,1]{0,3,2,4,1:T(8,128)(2,1)S(1)} %bitcast.42, f32[2048,16,2,32]{0,3,2,1:T(8,128)S(1)} %fusion.25), kind=kOutput, calls=%fused_computation.2 | convolution fusion | flops 1610612736 | bytes 12845056 | tf_op jit(solution)/shard_map/gnpi,gnqj->npiqj/dot_general | solution.py:27
  260.2 0.1 fusion.8
  260.2 0.2 copy.34
  260.4 0.2 copy.33
  260.6 0.4 fusion.9
  261.0 0.4 fusion.10
  261.4 0.4 fusion.5
  261.9 0.4 fusion.6
  262.3 0.7 maximum_multiply_fusion
  263.0 0.0 all-reduce.2.cloned.1.call-update
  263.0 125.1 %all-reduce.2.cloned.1.call-done = f32[2,8,32,32]{3,1,2,0:T(8,128)} async-done(((f32[2,8,32,32]{3,1,2,0:T(8,128)}), f32[2,8,32,32]{3,1,2,0:T(8,128)}) %all-reduce.2.cloned.1.call-update) | async-done | bytes 65552 | tf_op jit(solution)/shard_map/psum | solution.py:55
  388.1 1.7 copy.37
  (2 shorter events, 0.0 us)
Async XLA Ops:
  6.5 7.4 %copy-start.1 = (f32[256]{0:T(256)S(1)}, f32[256]{0:T(256)}, u32[]{:S(2)}) copy-start(f32[256]{0:T(256)} %param.8) | copy-start | bytes 3076
  6.5 7.4 %copy-start.2 = (s32[256]{0:T(256)S(1)}, s32[256]{0:T(256)}, u32[]{:S(2)}) copy-start(s32[256]{0:T(256)} %param.11) | copy-start | bytes 3076
  6.5 7.5 %copy-start.3 = (s32[32]{0:T(128)S(1)}, s32[32]{0:T(128)}, u32[]{:S(2)}) copy-start(s32[32]{0:T(128)} %param.10) | copy-start | bytes 388
  6.5 7.7 %copy-start.4 = (f32[8]{0:T(128)S(1)}, f32[8]{0:T(128)}, u32[]{:S(2)}) copy-start(f32[8]{0:T(128)} %param.9) | copy-start | bytes 100
  6.5 197.3 %all-gather.6.cloned.1.call-start = ((), (), s32[]{:S(2)}) async-start(), calls=%async_computation.2 | async-start | bytes 17825792 | tf_op jit(solution)/shard_map/all_gather | solution.py:46
  7.3 219.0 %all-gather.4.cloned.1.call-start = ((), (), s32[]{:S(2)}) async-start(), calls=%async_computation | async-start | bytes 12582912 | tf_op jit(solution)/shard_map/all_gather | solution.py:44
  13.8 374.3 %all-reduce.2.cloned.1.call-start = ((), (), s32[]{:S(2)}) async-start(), calls=%async_computation.1 | async-start | bytes 524288 | tf_op jit(solution)/shard_map/psum | solution.py:55
  226.3 23.5 %copy-start = (bf16[2048,1024]{0,1:T(8,128)(2,1)S(1)}, bf16[2048,1024]{0,1:T(8,128)(2,1)}, u32[]{:S(2)}) copy-start(bf16[2048,1024]{0,1:T(8,128)(2,1)} %copy.30) | copy-start | bytes 12582916
Sparse Core Ops, SparseCore 0:
  10.1 193.7 all-gather.5
  205.4 18.0 all-gather.3
  263.2 124.9 all-reduce.1
